TPU v7x, 32 devices: a whole 2x2x4 slice. The times are simulated.
32 devices in a mesh: row: 4 (over y, core), col: 8 (over z, x).
Axes of the slice: x: 2, y: 2, z: 4, core: 2. Of those that a mesh axis runs over, the one named last changes fastest.
Arguments:
- parent_front: float32 [8, 1024, 4, 2048], P(None, 'row', None, 'col'), may hold values from -6 to 6
- generators: bfloat16 [48, 256, 256], P('row'), may hold values from -1.5 to 1.5
- diagonal_blocks: bfloat16 [48, 256, 256], P('row'), may hold values from -6 to 6
- coupling: bfloat16 [2, 256, 256], replicated, may hold values from -0.375 to 0.375
- block_map: int32 [2, 24], replicated, may hold values from 0 to 31, as said below
- valid_rows: int32 [2, 24], replicated, may hold values from 128 to 256
Outputs:
- assembled: float32 [8, 1024, 4, 2048], P(None, 'row', None, 'col')
Inputs may be any that keep to these rules, and one draw needn't show every extreme that they name: `block_map`: for each child c and each s < 2, the child blocks s * 12 to (s + 1) * 12 - 1 map in increasing order to distinct parent blocks of the range s * 16 to (s + 1) * 16 - 1, and the parent blocks s * 16 + m * 4 of that range always receive one.
All inputs are finite; a program needn't handle non-finite values.
Results may differ from a plain program's by a relative error of at most 0.0028.
Values may be sent and summed in bfloat16 or wider, within the bound.
A program may use at most 128 MiB of HBM per device.

v0:
```python
import jax
import jax.numpy as jnp
from jax import lax
from jax.sharding import PartitionSpec as P


def split_children(stacked, half_rows):
    grouped = stacked.reshape((half_rows, 2, -1) + stacked.shape[2:])
    grouped = jnp.swapaxes(grouped, 0, 1)
    return grouped.reshape((2, -1) + stacked.shape[2:])


def shards(parent_front, generators, diagonal_blocks, coupling, block_map, valid_rows):
    row_count = lax.axis_size("row")
    col_count = lax.axis_size("col")
    half_rows = row_count // 2
    row_index = lax.axis_index("row")
    col_index = lax.axis_index("col")
    own_child = row_index % 2
    own_group = row_index // 2
    group_blocks = generators.shape[0]
    block_size = generators.shape[1]
    rank_width = generators.shape[2]
    rows_local = parent_front.shape[0]
    cols_local = parent_front.shape[2]
    window = 2 * rows_local
    row_cap = window // row_count
    col_cap = window // col_count
    map_child = lax.dynamic_index_in_dim(block_map, own_child, 0, keepdims=False)
    count_child = lax.dynamic_index_in_dim(valid_rows, own_child, 0, keepdims=False)
    coupling_own = lax.dynamic_index_in_dim(coupling, own_child, 0, keepdims=False)
    group_start = own_group * group_blocks
    map_group = lax.dynamic_slice_in_dim(map_child, group_start, group_blocks)
    count_group = lax.dynamic_slice_in_dim(count_child, group_start, group_blocks)
    row_offsets = jnp.arange(block_size, dtype=jnp.int32)
    kept_mask = (row_offsets[None, :] < count_group[:, None]).astype(jnp.bfloat16)
    masked = generators * kept_mask[:, :, None]
    projected = jnp.einsum(
        "ixq,qr->ixr", masked, coupling_own, preferred_element_type=jnp.float32
    ).astype(jnp.bfloat16)
    diag_kept = diagonal_blocks * kept_mask[:, :, None] * kept_mask[:, None, :]
    window_pos = map_group - own_group * window
    slot_ids = jnp.arange(window, dtype=jnp.int32)
    window_place = (window_pos[None, :] == slot_ids[:, None]).astype(jnp.bfloat16)
    row_place = window_place.reshape(row_cap, row_count, group_blocks)
    row_send = jnp.einsum(
        "kri,ixq->rkxq", row_place, masked, preferred_element_type=jnp.float32
    ).astype(jnp.bfloat16)
    row_received = lax.all_to_all(row_send, "row", split_axis=0, concat_axis=0, tiled=True)
    row_received = split_children(row_received, half_rows)
    wanted = jnp.arange(col_cap, dtype=jnp.int32) * col_count + col_index
    column_pick = (window_pos[None, :] == wanted[:, None]).astype(jnp.bfloat16)
    col_send = jnp.einsum(
        "ki,izq->kzq", column_pick, projected, preferred_element_type=jnp.float32
    ).astype(jnp.bfloat16)
    diag_send = jnp.einsum(
        "ki,ixz->kxz", column_pick, diag_kept, preferred_element_type=jnp.float32
    ).astype(jnp.bfloat16)
    col_received, diag_received = (
        lax.all_gather(col_send, "row", axis=0, tiled=True),
        lax.all_gather(diag_send, "row", axis=0, tiled=True),
    )
    col_received = split_children(
        col_received.reshape(row_count, col_cap, block_size, rank_width), half_rows
    )
    diag_received = split_children(
        diag_received.reshape(row_count, col_cap, block_size, block_size), half_rows
    )
    row_parents = jnp.arange(rows_local, dtype=jnp.int32) * row_count + row_index
    col_parents = jnp.arange(cols_local, dtype=jnp.int32) * col_count + col_index
    on_diag = (row_parents[:, None] == col_parents[None, :]).astype(jnp.float32)
    running = parent_front
    for child_index in range(2):
        child_tile = jnp.einsum(
            "axq,bzq->axbz",
            row_received[child_index],
            col_received[child_index],
            preferred_element_type=jnp.float32,
        )
        diag_part = diag_received[child_index].astype(jnp.float32).transpose(1, 0, 2)
        child_tile = child_tile + on_diag[:, None, :, None] * diag_part[None]
        rounded = lax.optimization_barrier(child_tile.astype(jnp.bfloat16))
        running = running + rounded.astype(jnp.float32)
    return running


def solution(mesh):
    in_specs = (
        P(None, "row", None, "col"),
        P("row", None, None),
        P("row", None, None),
        P(),
        P(),
        P(),
    )
    out_specs = P(None, "row", None, "col")
    return jax.shard_map(shards, mesh=mesh, in_specs=in_specs, out_specs=out_specs, check_vma=False)
```

profile of v0, /device:TPU:1, one launch (start us, length us, event | category | flops | bytes accessed | tf_op | source)
XLA Modules:
  0.0 94.3 jit_solution(12335367808657521242)
XLA Ops:
  6.5 0.8 subtract_bitcast_fusion
  7.5 2.0 %fusion.8 = bf16[12,256,256]{2,1,0:T(8,128)(2,1)S(1)} fusion(bf16[12,256,256]{2,1,0:T(8,128)(2,1)} %param.7, bf16[12,256]{1,0:T(8,128)(2,1)S(1)} %fusion.17, bf16[2,256,256]{2,1,0:T(8,128)(2,1)S(1)} %copy-done, s32[]{:T(128)S(6)} %select_n.27), kind=kOutput, calls=%fused_computation.13 | convolution fusion | flops 403439616 | bytes 3284996 | tf_op jit(solution)/shard_map/ixq,qr->ixr/dot_general | solution.py:38
  9.6 1.0 %fusion.13 = bf16[2,256,256]{2,0,1:T(2,128)(2,1)S(1)} fusion(bf16[12,256,256]{2,1,0:T(8,128)(2,1)S(1)} %fusion.8, s32[12]{0:T(128)S(1)} %get-tuple-element.13, s32[2]{0:T(128)S(1)} %multiply_add_fusion.3), kind=kOutput, calls=%fused_computation.17 | convolution fusion | flops 3276824 | bytes 1835064 | tf_op jit(solution)/shard_map/ki,izq->kzq/dot_general | solution.py:53
  10.6 0.7 copy.20
  11.4 1.7 %multiply_bitcast_fusion = (bf16[12,256,256,1]{2,1,0,3:T(8,128)(2,1)S(1)}, bf16[12,256,256]{2,1,0:T(8,128)(2,1)S(1)}) fusion(bf16[12,256,256]{2,1,0:T(8,128)(2,1)S(1)} %copy-done.1, bf16[12,256]{1,0:T(8,128)(2,1)S(1)} %fusion.17, bf16[12,256,256]{2,1,0:T(8,128)(2,1)} %param.8), kind=kLoop, calls=%fused_computation.15 | loop fusion | flops 2359296 | bytes 6297600 | tf_op jit(solution)/shard_map/mul | solution.py:37
  13.2 1.0 %fusion.10 = bf16[2,256,256]{2,0,1:T(2,128)(2,1)S(1)} fusion(bf16[12,256,256]{2,1,0:T(8,128)(2,1)S(1)} %get-tuple-element.12, s32[12]{0:T(128)S(1)} %get-tuple-element.13, s32[2]{0:T(128)S(1)} %multiply_add_fusion.3), kind=kOutput, calls=%fused_computation.16 | convolution fusion | flops 3276824 | bytes 1835064 | tf_op jit(solution)/shard_map/ki,ixz->kxz/dot_general | solution.py:56
  14.2 0.7 copy.23
  15.0 1.5 %convert_bitcast_fusion = bf16[4,4,256,256]{3,0,1,2:T(4,128)(2,1)S(1)} fusion(bf16[12,256,256,1]{2,1,0,3:T(8,128)(2,1)S(1)} %get-tuple-element.11, s32[4,4]{1,0:T(4,128)S(1)} %multiply_add_fusion, s32[12]{0:T(128)S(1)} %get-tuple-element.13), kind=kOutput, calls=%fused_computation.11 | convolution fusion | flops 26214592 | bytes 3670128 | tf_op jit(solution)/shard_map/kri,ixq->rkxq/dot_general | solution.py:46
  16.5 2.1 %copy.18 = bf16[4,4,256,256]{3,1,2,0:T(4,128)(2,1)} copy(bf16[4,4,256,256]{3,0,1,2:T(4,128)(2,1)S(1)} %convert_bitcast_fusion) | data formatting | bytes 4194304 | tf_op jit(solution)/shard_map/convert_element_type | solution.py:48
  18.6 4.3 %all-to-all-start = ((bf16[4,4,256,256]{3,1,2,0:T(4,128)(2,1)}), bf16[4,4,256,256]{3,1,2,0:T(4,128)(2,1)S(1)}, u32[]{:S(2)}, u32[]{:S(2)}) async-start(bf16[4,4,256,256]{3,1,2,0:T(4,128)(2,1)} %copy.18), calls=%async_computation | async-start | bytes 4194304 | tf_op jit(solution)/shard_map/all_to_all | solution.py:49
  23.0 10.8 %all-gather.3.cloned.1.call-done = bf16[8,256,256]{2,1,0:T(8,128)(2,1)} async-done(((bf16[2,256,256]{2,1,0:T(8,128)(2,1)}), bf16[8,256,256]{2,1,0:T(8,128)(2,1)}) %all-gather.3.cloned.1.call-update) | async-done | bytes 1048592 | tf_op jit(solution)/shard_map/all_gather | solution.py:60
  33.8 1.3 %copy.50 = bf16[2,2,2,256,256]{4,3,2,0,1:T(8,128)(2,1)S(1)} copy(bf16[2,2,2,256,256]{4,3,2,1,0:T(8,128)(2,1)} %bitcast.64) | data formatting | bytes 2097152 | tf_op jit(solution)/shard_map/reshape;reshape | solution.py:8
  35.1 1.1 %fusion.32 = (bf16[1,2,2,256,256]{4,3,2,1,0:T(8,128)(2,1)}, bf16[1,2,2,256,256]{4,3,2,1,0:T(8,128)(2,1)}) fusion(bf16[2,2,2,256,256]{4,3,2,1,0:T(8,128)(2,1)S(1)} %bitcast.63), kind=kLoop, calls=%fused_computation.47 | loop fusion | bytes 2097152 | tf_op jit(solution)/shard_map/slice | solution.py:77
  36.2 21.1 %all-gather.5.cloned.1.call-done = bf16[8,256,256]{2,1,0:T(8,128)(2,1)} async-done(((bf16[2,256,256]{2,1,0:T(8,128)(2,1)}), bf16[8,256,256]{2,1,0:T(8,128)(2,1)}) %all-gather.5.cloned.1.call-update) | async-done | bytes 1048592 | tf_op jit(solution)/shard_map/all_gather | solution.py:61
  57.2 1.3 %fusion.33 = (bf16[1,2,2,256,256]{4,3,2,0,1:T(8,128)(2,1)S(1)}, bf16[1,2,2,256,256]{4,3,2,0,1:T(8,128)(2,1)S(1)}) fusion(bf16[2,2,2,256,256]{4,3,2,0,1:T(8,128)(2,1)} %bitcast.65), kind=kLoop, calls=%fused_computation.48 | loop fusion | bytes 2097152 | tf_op jit(solution)/shard_map/slice | solution.py:80
  58.5 0.4 copy.49
  58.9 0.1 fusion.31
  59.1 0.1 convert_bitcast_fusion.2
  59.2 0.1 convert_bitcast_fusion.1
  59.3 0.8 copy-done.3
  60.1 1.3 %add_convert_fusion = bf16[8,256,4,256]{3,1,2,0:T(8,128)(2,1)S(1)} fusion(f32[256,4,256]{2,0,1:T(8,128)S(1)} %convert_bitcast_fusion.1, f32[8,4]{1,0:T(8,128)S(1)} %compare_convert_fusion, bf16[8,256,256,1]{2,1,3,0:T(8,128)(2,1)S(1)} %bitcast.67, bf16[4,256,256,1]{2,1,0,3:T(8,128)(2,1)S(1)} %bitcast.69), kind=kOutput, calls=%fused_computation.2 | convolution fusion | flops 1080033280 | bytes 6815872 | tf_op jit(solution)/shard_map/axq,bzq->axbz/dot_general | solution.py:74
  61.4 3.4 %add_convert_fusion.1 = bf16[8,256,4,256]{3,1,2,0:T(8,128)(2,1)} fusion(f32[256,4,256]{2,0,1:T(8,128)S(1)} %convert_bitcast_fusion.2, f32[8,4]{1,0:T(8,128)S(1)} %compare_convert_fusion, bf16[8,256,256,1]{2,1,3,0:T(8,128)(2,1)S(1)} %bitcast.66, bf16[4,256,256,1]{2,1,0,3:T(8,128)(2,1)S(1)} %bitcast.68), kind=kOutput, calls=%fused_computation.3 | convolution fusion | flops 1080033280 | bytes 6815872 | tf_op jit(solution)/shard_map/axq,bzq->axbz/dot_general | solution.py:74
  64.8 10.5 %fusion = f32[8,256,4,256]{3,1,2,0:T(8,128)} fusion(f32[8,256,4,256]{3,2,1,0:T(4,128)} %param.6, bf16[8,256,4,256]{3,1,2,0:T(8,128)(2,1)S(1)} %add_convert_fusion, bf16[8,256,4,256]{3,1,2,0:T(8,128)(2,1)} %add_convert_fusion.1), kind=kLoop, calls=%fused_computation.1 | loop fusion | flops 8388608 | bytes 25165824 | tf_op jit(solution)/shard_map/add | solution.py:83
  75.3 12.2 %copy.25 = f32[8,256,4,256]{3,2,1,0:T(4,128)} copy(f32[8,256,4,256]{3,1,2,0:T(8,128)} %fusion) | data formatting | bytes 16777216 | tf_op jit(solution)/shard_map/add | solution.py:83
  (18 shorter events, 0.3 us)
Async XLA Ops:
  6.5 1.0 %copy-start = (bf16[2,256,256]{2,1,0:T(8,128)(2,1)S(1)}, bf16[2,256,256]{2,1,0:T(8,128)(2,1)}, u32[]{:S(2)}) copy-start(bf16[2,256,256]{2,1,0:T(8,128)(2,1)} %param.9) | copy-start | bytes 786436
  6.5 27.3 %all-gather.3.cloned.1.call-start = ((), (), s32[]{:S(2)}) async-start(), calls=%async_computation.1 | async-start | bytes 1310720 | tf_op jit(solution)/shard_map/all_gather | solution.py:60
  9.6 1.9 %copy-start.1 = (bf16[12,256,256]{2,1,0:T(8,128)(2,1)S(1)}, bf16[12,256,256]{2,1,0:T(8,128)(2,1)}, u32[]{:S(2)}) copy-start(bf16[12,256,256]{2,1,0:T(8,128)(2,1)} %param.7) | copy-start | bytes 4718596
  11.4 45.9 %all-gather.5.cloned.1.call-start = ((), (), s32[]{:S(2)}) async-start(), calls=%async_computation.2 | async-start | bytes 1310720 | tf_op jit(solution)/shard_map/all_gather | solution.py:61
  18.6 39.9 %all-to-all-start = ((bf16[4,4,256,256]{3,1,2,0:T(4,128)(2,1)}), bf16[4,4,256,256]{3,1,2,0:T(4,128)(2,1)S(1)}, u32[]{:S(2)}, u32[]{:S(2)}) async-start(bf16[4,4,256,256]{3,1,2,0:T(4,128)(2,1)} %copy.18), calls=%async_computation | async-start | bytes 4194304 | tf_op jit(solution)/shard_map/all_to_all | solution.py:49
  59.0 1.0 %copy-start.3 = (bf16[1,2,2,256,256]{4,3,2,1,0:T(8,128)(2,1)S(1)}, bf16[1,2,2,256,256]{4,3,2,1,0:T(8,128)(2,1)}, u32[]{:S(2)}) copy-start(bf16[1,2,2,256,256]{4,3,2,1,0:T(8,128)(2,1)} %get-tuple-element.8) | copy-start | bytes 1572868
  60.1 1.3 %copy-start.2 = (bf16[1,2,2,256,256]{4,3,2,1,0:T(8,128)(2,1)S(1)}, bf16[1,2,2,256,256]{4,3,2,1,0:T(8,128)(2,1)}, u32[]{:S(2)}) copy-start(bf16[1,2,2,256,256]{4,3,2,1,0:T(8,128)(2,1)} %get-tuple-element.7) | copy-start | bytes 1572868
Sparse Core Ops, SparseCore 0:
  11.5 22.2 all-gather.2
  35.4 21.8 all-gather.4
where the time goes:
time: 95 us; the launch traced here: 94.3 us
  waiting for transfers between devices  32 us (34%)
  local copies, waits for them, and re-layouts  20.8 us (22%)
  between operations  13.5 us (14%)
  other arithmetic  13.4 us (14%)
  matrix products  10.3 us (11%)
  starting transfers between devices  4.32 us (5%)
    all_gather x1, waiting for transfers between devices, shards(): lax.all_gather(diag_send, 'row', axis=0, tiled=True)  21.1 us
    add x1, local copies, waits for them, and re-layouts, shards(): running = running + rounded.astype(jnp.float32)  12.2 us
    all_gather x1, waiting for transfers between devices, shards(): lax.all_gather(col_send, 'row', axis=0, tiled=True)  10.8 us
    add x1, other arithmetic, shards(): running = running + rounded.astype(jnp.float32)  10.5 us
    dot_general x2, matrix products, shards(): jnp.einsum('axq,bzq->axbz', row_received[child_index], col_received[child...  4.72 us
    all_to_all x1, starting transfers between devices, shards(): lax.all_to_all(row_send, 'row', split_axis=0, concat_axis=0, tiled=True)  4.28 us
    convert_element_type x1, local copies, waits for them, and re-layouts, shards(): row_send = jnp.einsum('kri,ixq->rkxq', row_place, masked, preferred_eleme...  2.13 us
    dot_general x1, matrix products, shards(): jnp.einsum('ixq,qr->ixr', masked, coupling_own, preferred_element_type=jn...  2.03 us
  transfers between devices with their start and end apart: 3, of which 2 were waited for; matrix products, arithmetic and copies ran while one was open for 11% of the time, Pallas kernels for 0%

commit v1 on v0

v1 whole, which is shorter than its diff:
```python
import functools

import jax
import jax.numpy as jnp
from jax import lax
from jax.experimental import pallas as pl
from jax.experimental.pallas import tpu as pltpu
from jax.sharding import PartitionSpec as P

MESH = pl.DeviceIdType.MESH
QUAD = 4


def exchange_kernel(
    row_count, col_count, row_cap, col_cap,
    gen_ref, diag_ref, coupling_ref, map_ref, count_ref,
    rows_out, cols_out, diag_out,
    send_rows, send_pair, rows_raw, cols_raw, diag_raw,
    far_send, far_recv, quad_send, quad_recv, pair_send, pair_recv,
    col_send, col_recv, fwd_send, fwd_recv, diag_send, diag_recv,
):
    groups = row_count // 2
    group_blocks, block, rank = gen_ref.shape
    window = row_cap * row_count
    chunk = row_cap * block // QUAD
    row = lax.axis_index("row")
    col = lax.axis_index("col")
    group = row // 2
    core = row % 2
    quarter = col % QUAD
    pair_row = group * 2 + 1 - core
    diag_row = col % row_count
    quad_cols = (
        col + 1 - 2 * (quarter % 2),
        col + 2 - 4 * (quarter // 2),
        col + 3 - 2 * quarter,
    )

    def lookup(child, source, slot):
        found = jnp.int32(0)
        count = jnp.int32(0)
        target = source * window + slot
        for k in range(group_blocks):
            hit = map_ref[child, source * group_blocks + k] == target
            found = jnp.where(hit, k, found)
            count = jnp.where(hit, count_ref[child, source * group_blocks + k], count)
        return found, count

    def remote(src, dst, send, recv, to_row, to_col):
        return pltpu.make_async_remote_copy(
            src_ref=src, dst_ref=dst, send_sem=send, recv_sem=recv,
            device_id=(to_row, to_col), device_id_type=MESH,
        )

    barrier = pltpu.get_barrier_semaphore()
    for k in range(1, row_count):
        pl.semaphore_signal(
            barrier, inc=1, device_id=((row + k) % row_count, col), device_id_type=MESH
        )
    for other in quad_cols:
        pl.semaphore_signal(barrier, inc=1, device_id=(row, other), device_id_type=MESH)

    start_row = quarter * chunk
    quarter_slot = start_row // block
    quarter_off = pl.multiple_of(start_row % block, chunk)
    for k in range(1, groups):
        dest = (group + k) % groups
        for r in range(2):
            found, _ = lookup(core, group, quarter_slot * row_count + 2 * dest + r)
            send_rows[k - 1, r] = gen_ref[found, pl.ds(quarter_off, chunk), :]
    for t in range(col_cap):
        found, _ = lookup(core, group, t * col_count + col)
        cols_raw[core, group, pl.ds(t * block, block), :] = gen_ref[found]
        diag_raw[core, group, pl.ds(t * block, block), :] = diag_ref[found]

    pl.semaphore_wait(barrier, row_count - 1 + QUAD - 1)

    sends = []

    def far_copy(k, r, child, source, dest_row):
        return remote(
            send_rows.at[k - 1, r], rows_raw.at[child, source, quarter],
            far_send.at[k - 1, r], far_recv.at[k - 1, child], dest_row, col,
        )

    for k in range(1, groups):
        dest = (group + k) % groups
        for r in range(2):
            copy = far_copy(k, r, core, group, 2 * dest + r)
            copy.start()
            sends.append(copy)

    own_cols = cols_raw.at[core, group]
    for k in range(1, groups):
        dest = (group + k) % groups
        copy = remote(own_cols, own_cols, col_send.at[k], col_recv.at[k], 2 * dest + core, col)
        copy.start()
        sends.append(copy)
    copy = remote(own_cols, own_cols, col_send.at[0], col_recv.at[0], pair_row, col)
    copy.start()
    sends.append(copy)

    own_diag = diag_raw.at[core, group]
    diag_away = remote(
        own_diag, own_diag, diag_send, diag_recv.at[core, group], diag_row, col
    )

    @pl.when(row != diag_row)
    def _():
        diag_away.start()

    for m in range(row_cap):
        found, _ = lookup(core, group, m * row_count + pair_row)
        send_pair[pl.ds(m * block, block), :] = gen_ref[found]
    for j in range(QUAD):
        slot, off = j * chunk // block, j * chunk % block
        found, _ = lookup(core, group, slot * row_count + row)
        rows_raw[core, group, j] = gen_ref[found, off:off + chunk, :]
    for j in range(QUAD):
        copy = remote(
            send_pair.at[pl.ds(j * chunk, chunk)], rows_raw.at[core, group, j],
            pair_send.at[j], pair_recv.at[j], pair_row, col,
        )
        copy.start()
        sends.append(copy)

    row_iota = lax.broadcasted_iota(jnp.int32, (block, rank), 0)
    col_iota = lax.broadcasted_iota(jnp.int32, (block, block), 1)

    def finish_rows(child, source, j):
        slot, off = j * chunk // block, j * chunk % block
        _, count = lookup(child, source, slot * row_count + row)
        kept = (row_iota[off:off + chunk] < count).astype(jnp.float32).astype(jnp.bfloat16)
        rows_out[source, j, :, child * rank:(child + 1) * rank] = rows_raw[child, source, j] * kept

    def finish_cols(child, source):
        for t in range(col_cap):
            _, count = lookup(child, source, t * col_count + col)
            kept = (row_iota < count).astype(jnp.float32).astype(jnp.bfloat16)
            masked = cols_raw[child, source, t * block:(t + 1) * block, :] * kept
            cols_out[source, t, :, child * rank:(child + 1) * rank] = jnp.dot(
                masked, coupling_ref[child], preferred_element_type=jnp.float32
            ).astype(jnp.bfloat16)

    for k in range(1, groups):
        source = (group + groups - k) % groups
        for child in range(2):
            far_copy(k, 0, child, source, row).wait_recv()
            landed = rows_raw.at[child, source, quarter]
            for j, other in enumerate(quad_cols):
                copy = remote(
                    landed, landed, quad_send.at[k - 1, child, j], quad_recv.at[k - 1, child, j],
                    row, other,
                )
                copy.start()
                sends.append(copy)

    for j in range(QUAD):
        remote(
            send_pair.at[pl.ds(j * chunk, chunk)], rows_raw.at[1 - core, group, j],
            pair_send.at[j], pair_recv.at[j], pair_row, col,
        ).wait_recv()
    for child in range(2):
        for j in range(QUAD):
            finish_rows(child, group, j)
    remote(own_cols, cols_raw.at[1 - core, group], col_send.at[0], col_recv.at[0], pair_row, col).wait_recv()
    for child in range(2):
        finish_cols(child, group)

    for k in range(1, groups):
        source = (group + groups - k) % groups
        landed = cols_raw.at[core, source]
        remote(own_cols, landed, col_send.at[k], col_recv.at[k], pair_row, col).wait_recv()
        copy = remote(landed, landed, fwd_send.at[k - 1], fwd_recv.at[k - 1], pair_row, col)
        copy.start()
        sends.append(copy)
    for k in range(1, groups):
        source = (group + groups - k) % groups
        remote(
            own_cols, cols_raw.at[1 - core, source], fwd_send.at[k - 1], fwd_recv.at[k - 1], pair_row, col
        ).wait_recv()
        for child in range(2):
            finish_cols(child, source)

    @pl.when(row == diag_row)
    def _():
        for source in range(groups):
            for child in range(2):
                @pl.when(2 * source + child != row)
                def _():
                    remote(
                        own_diag, diag_raw.at[child, source], diag_send, diag_recv.at[child, source],
                        pair_row, col,
                    ).wait_recv()
        for source in range(groups):
            for t in range(col_cap):
                total = jnp.zeros((block, block), jnp.float32)
                for child in range(2):
                    _, count = lookup(child, source, t * col_count + col)
                    inside = jnp.maximum(row_iota, col_iota) < count
                    piece = diag_raw[child, source, t * block:(t + 1) * block, :].astype(jnp.float32)
                    total = total + jnp.where(inside, piece, 0.0)
                diag_out[source, t] = total

    @pl.when(row != diag_row)
    def _():
        diag_out[...] = jnp.zeros_like(diag_out)

    for k in range(1, groups):
        source = (group + groups - k) % groups
        for child in range(2):
            for j, other in enumerate(quad_cols):
                landed = rows_raw.at[child, source, other % QUAD]
                remote(
                    landed, landed, quad_send.at[k - 1, child, j], quad_recv.at[k - 1, child, j],
                    row, other,
                ).wait_recv()
        for child in range(2):
            for j in range(QUAD):
                finish_rows(child, source, j)

    for copy in sends:
        copy.wait_send()

    @pl.when(row != diag_row)
    def _():
        diag_away.wait_send()


def shards(parent_front, generators, diagonal_blocks, coupling, block_map, valid_rows):
    row_count = lax.axis_size("row")
    col_count = lax.axis_size("col")
    groups = row_count // 2
    block, rank = generators.shape[1:]
    rows_local = parent_front.shape[0]
    cols_local = parent_front.shape[2]
    row_cap = rows_local // groups
    col_cap = cols_local // groups
    chunk = row_cap * block // QUAD
    vmem = pl.BlockSpec(memory_space=pltpu.VMEM)
    smem = pl.BlockSpec(memory_space=pltpu.SMEM)
    dma = pltpu.SemaphoreType.DMA
    rows, cols, diag = pl.pallas_call(
        functools.partial(exchange_kernel, row_count, col_count, row_cap, col_cap),
        out_shape=(
            jax.ShapeDtypeStruct((groups, QUAD, chunk, 2 * rank), jnp.bfloat16),
            jax.ShapeDtypeStruct((groups, col_cap, block, 2 * rank), jnp.bfloat16),
            jax.ShapeDtypeStruct((groups, col_cap, block, block), jnp.float32),
        ),
        in_specs=[vmem, vmem, vmem, smem, smem],
        out_specs=(vmem, vmem, vmem),
        scratch_shapes=[
            pltpu.VMEM((groups - 1, 2, chunk, rank), jnp.bfloat16),
            pltpu.VMEM((row_cap * block, rank), jnp.bfloat16),
            pltpu.VMEM((2, groups, QUAD, chunk, rank), jnp.bfloat16),
            pltpu.VMEM((2, groups, col_cap * block, rank), jnp.bfloat16),
            pltpu.VMEM((2, groups, col_cap * block, block), jnp.bfloat16),
            dma((groups - 1, 2)),
            dma((groups - 1, 2)),
            dma((groups - 1, 2, QUAD - 1)),
            dma((groups - 1, 2, QUAD - 1)),
            dma((QUAD,)),
            dma((QUAD,)),
            dma((groups,)),
            dma((groups,)),
            dma((groups - 1,)),
            dma((groups - 1,)),
            dma,
            dma((2, groups)),
        ],
        compiler_params=pltpu.CompilerParams(
            collective_id=0, has_side_effects=True, vmem_limit_bytes=48 * 1024 * 1024
        ),
    )(generators, diagonal_blocks, coupling, block_map, valid_rows)
    rows = rows.reshape(rows_local, block, 2 * rank)
    cols = cols.reshape(cols_local, block, 2 * rank)
    diag = diag.reshape(cols_local, block, block)
    row_parents = jnp.arange(rows_local, dtype=jnp.int32) * row_count + lax.axis_index("row")
    col_parents = jnp.arange(cols_local, dtype=jnp.int32) * col_count + lax.axis_index("col")
    on_diag = (row_parents[:, None] == col_parents[None, :]).astype(jnp.float32)
    tiles = jnp.einsum("axq,bzq->axbz", rows, cols, preferred_element_type=jnp.float32)
    placed = on_diag[:, None, :, None] * diag.transpose(1, 0, 2)[None]
    return parent_front + (tiles + placed)


def solution(mesh):
    in_specs = (
        P(None, "row", None, "col"),
        P("row", None, None),
        P("row", None, None),
        P(),
        P(),
        P(),
    )
    out_specs = P(None, "row", None, "col")
    return jax.shard_map(shards, mesh=mesh, in_specs=in_specs, out_specs=out_specs, check_vma=False)
```

time: 95 us -> 53.6 us (0.56)
  waiting for transfers between devices: 32 us -> 0 us
  Pallas kernels: 0 us -> 25 us
  between operations: 13.5 us -> 0.02 us
  other arithmetic: 13.4 us -> 0.08 us
  starting transfers between devices: 4.32 us -> 0 us
  local copies, waits for them, and re-layouts: 20.8 us -> 17.3 us
    all_gather x2 -> x0, waiting for transfers between devices: 31.9 us -> none  [the longest x1 21.1 us: shards(): lax.all_gather(diag_send, 'row', axis=0, tiled=True)]
    pallas_call x0 -> x1, Pallas kernels: none -> 25 us  [shards(): pl.pallas_call(functools.partial(exchange_kernel, row_count, col_count, r...]
    add x4 -> x2, other arithmetic: 10.5 us -> 0.01 us  [the longest x1 0.01 us: shards(): jnp.arange(rows_local, dtype=jnp.int32) * row_count + lax.axis_index('row')]
    all_to_all x1 -> x0, starting transfers between devices: 4.28 us -> none  [shards(): lax.all_to_all(row_send, 'row', split_axis=0, concat_axis=0, tiled=True)]
    unnamed x8 -> x10, local copies, waits for them, and re-layouts: 0.88 us -> 5.12 us
    convert_element_type x3 -> x0, local copies, waits for them, and re-layouts: 3.62 us -> none  [the longest x1 2.13 us: shards(): row_send = jnp.einsum('kri,ixq->rkxq', row_place, masked, preferred_eleme...]
    slice x3 -> x0, local copies, waits for them, and re-layouts: 2.47 us -> none  [the longest x1 1.27 us: shards(): diag_received[child_index].astype(jnp.float32).transpose(1, 0, 2)]
    mul x1 -> x0, other arithmetic: 1.72 us -> none  [shards(): masked = generators * kept_mask[:, :, None]]
  transfers between devices with their start and end apart: 3 -> 0, of which waited for: 2 -> 0; matrix products, arithmetic and copies ran while one was open for 11% -> 0% of each run, Pallas kernels for 0% -> 0%
where the time goes in v1:
time: 53.6 us; the launch traced here: 52.8 us
  Pallas kernels  25 us (47%)
  local copies, waits for them, and re-layouts  17.3 us (32%)
  matrix products  10.4 us (19%)
    pallas_call x1, Pallas kernels, shards(): pl.pallas_call(functools.partial(exchange_kernel, row_count, col_count, r...  25 us
    add x1, local copies, waits for them, and re-layouts, shards(): return parent_front + (tiles + placed)  12.2 us
    dot_general x1, matrix products, shards(): jnp.einsum('axq,bzq->axbz', rows, cols, preferred_element_type=jnp.float32)  10.4 us
    unnamed x10, local copies, waits for them, and re-layouts  5.12 us

profile of v1, /device:TPU:1, one launch (start us, length us, event | category | flops | bytes accessed | tf_op | source)
XLA Modules:
  0.0 52.8 jit_solution(12488665837932127686)
XLA Ops:
  0.0 0.1 compare_convert_fusion
  0.1 0.0 copy-start
  0.1 1.4 %copy-done = bf16[12,256,256]{2,1,0:T(8,128)(2,1)S(1)} copy-done((bf16[12,256,256]{2,1,0:T(8,128)(2,1)S(1)}, bf16[12,256,256]{2,1,0:T(8,128)(2,1)}, u32[]{:S(2)}) %copy-start) | copy-done | bytes 1572888
  1.5 0.0 copy-start.1
  1.5 1.4 %copy-done.1 = bf16[12,256,256]{2,1,0:T(8,128)(2,1)S(1)} copy-done((bf16[12,256,256]{2,1,0:T(8,128)(2,1)S(1)}, bf16[12,256,256]{2,1,0:T(8,128)(2,1)}, u32[]{:S(2)}) %copy-start.1) | copy-done | bytes 1572888
  2.9 0.0 copy-start.2
  2.9 0.9 %copy-done.2 = bf16[2,256,256]{2,1,0:T(8,128)(2,1)S(1)} copy-done((bf16[2,256,256]{2,1,0:T(8,128)(2,1)S(1)}, bf16[2,256,256]{2,1,0:T(8,128)(2,1)}, u32[]{:S(2)}) %copy-start.2) | copy-done | bytes 262168
  3.9 0.0 copy-start.3
  3.9 0.7 %copy-done.3 = s32[2,24]{1,0:T(2,128)S(1)} copy-done((s32[2,24]{1,0:T(2,128)S(1)}, s32[2,24]{1,0:T(2,128)}, u32[]{:S(2)}) %copy-start.3) | copy-done | bytes 216
  4.5 0.0 copy-start.4
  4.5 0.7 %copy-done.4 = s32[2,24]{1,0:T(2,128)S(1)} copy-done((s32[2,24]{1,0:T(2,128)S(1)}, s32[2,24]{1,0:T(2,128)}, u32[]{:S(2)}) %copy-start.4) | copy-done | bytes 216
  5.2 25.0 %shard_map.64 = (bf16[2,4,256,512]{3,2,1,0:T(8,128)(2,1)}, bf16[2,2,256,512]{3,2,1,0:T(8,128)(2,1)S(1)}, f32[2,2,256,256]{3,2,1,0:T(8,128)S(1)}) custom-call(bf16[12,256,256]{2,1,0:T(8,128)(2,1)S(1)} %copy-done, bf16[12,256,256]{2,1,0:T(8,128)(2,1)S(1)} %copy-done.1, bf16[2,256,256]{2,1,0:T(8,128)(2,1)S(1)} %copy-done.2, s32[2,24]{1,0:T(2,128)S(1)} %copy-done.3, ...), custom_call_target="tpu_custom_call" | custom-call | tf_op jit(solution)/shard_map/pallas_call | solution.py:243
  30.3 10.4 %copy_add_fusion = f32[8,256,4,256]{3,1,2,0:T(8,128)} fusion(f32[8,256,4,256]{3,2,1,0:T(4,128)} %param.6, f32[256,4,256]{2,0,1:T(8,128)S(1)} %bitcast.13, f32[8,4]{1,0:T(8,128)S(1)} %compare_convert_fusion, bf16[8,256,512,1]{2,1,3,0:T(8,128)(2,1)} %bitcast.15, bf16[4,256,512,1]{2,1,0,3:T(8,128)(2,1)S(1)} %bitcast.14), kind=kOutput, calls=%fused_computation | convolution fusion | flops 2153775104 | bytes 20971648 | tf_op jit(solution)/shard_map/axq,bzq->axbz/dot_general | solution.py:281
  40.7 12.2 %copy.8 = f32[8,256,4,256]{3,2,1,0:T(4,128)} copy(f32[8,256,4,256]{3,1,2,0:T(8,128)} %copy_add_fusion) | data formatting | bytes 16777216 | tf_op jit(solution)/shard_map/add | solution.py:283
  (2 shorter events, 0.0 us)
Async XLA Ops:
  0.1 1.4 %copy-start = (bf16[12,256,256]{2,1,0:T(8,128)(2,1)S(1)}, bf16[12,256,256]{2,1,0:T(8,128)(2,1)}, u32[]{:S(2)}) copy-start(bf16[12,256,256]{2,1,0:T(8,128)(2,1)} %gen_ref.1) | copy-start | bytes 4718596
  1.5 1.4 %copy-start.1 = (bf16[12,256,256]{2,1,0:T(8,128)(2,1)S(1)}, bf16[12,256,256]{2,1,0:T(8,128)(2,1)}, u32[]{:S(2)}) copy-start(bf16[12,256,256]{2,1,0:T(8,128)(2,1)} %diag_ref.1) | copy-start | bytes 4718596
  2.9 0.9 %copy-start.2 = (bf16[2,256,256]{2,1,0:T(8,128)(2,1)S(1)}, bf16[2,256,256]{2,1,0:T(8,128)(2,1)}, u32[]{:S(2)}) copy-start(bf16[2,256,256]{2,1,0:T(8,128)(2,1)} %coupling_ref.1) | copy-start | bytes 786436
  3.9 0.7 %copy-start.3 = (s32[2,24]{1,0:T(2,128)S(1)}, s32[2,24]{1,0:T(2,128)}, u32[]{:S(2)}) copy-start(s32[2,24]{1,0:T(2,128)} %map_ref.1) | copy-start | bytes 580
  4.5 0.7 %copy-start.4 = (s32[2,24]{1,0:T(2,128)S(1)}, s32[2,24]{1,0:T(2,128)}, u32[]{:S(2)}) copy-start(s32[2,24]{1,0:T(2,128)} %count_ref.1) | copy-start | bytes 580

commit v2 on v1

--- a/solution.py
+++ b/solution.py
@@ -9,12 +9,14 @@
 
 MESH = pl.DeviceIdType.MESH
 QUAD = 4
+LANES = 128
 
 
 def exchange_kernel(
     row_count, col_count, row_cap, col_cap,
-    gen_ref, diag_ref, coupling_ref, map_ref, count_ref,
+    gen_hbm, diag_hbm, coupling_hbm, map_hbm, count_hbm,
     rows_out, cols_out, diag_out,
+    gen_ref, diag_ref, coupling_ref, map_ref, count_ref, load_sem,
     send_rows, send_pair, rows_raw, cols_raw, diag_raw,
     far_send, far_recv, quad_send, quad_recv, pair_send, pair_recv,
     col_send, col_recv, fwd_send, fwd_recv, diag_send, diag_recv,
@@ -52,6 +54,16 @@
             device_id=(to_row, to_col), device_id_type=MESH,
         )
 
+    loads = [
+        pltpu.make_async_copy(src, dst, load_sem.at[n])
+        for n, (src, dst) in enumerate((
+            (map_hbm, map_ref), (count_hbm, count_ref), (gen_hbm, gen_ref),
+            (diag_hbm, diag_ref), (coupling_hbm, coupling_ref),
+        ))
+    ]
+    for load in loads:
+        load.start()
+
     barrier = pltpu.get_barrier_semaphore()
     for k in range(1, row_count):
         pl.semaphore_signal(
@@ -60,6 +72,8 @@
     for other in quad_cols:
         pl.semaphore_signal(barrier, inc=1, device_id=(row, other), device_id_type=MESH)
 
+    for load in loads:
+        load.wait()
     start_row = quarter * chunk
     quarter_slot = start_row // block
     quarter_off = pl.multiple_of(start_row % block, chunk)
@@ -138,8 +152,9 @@
             _, count = lookup(child, source, t * col_count + col)
             kept = (row_iota < count).astype(jnp.float32).astype(jnp.bfloat16)
             masked = cols_raw[child, source, t * block:(t + 1) * block, :] * kept
-            cols_out[source, t, :, child * rank:(child + 1) * rank] = jnp.dot(
-                masked, coupling_ref[child], preferred_element_type=jnp.float32
+            cols_out[source, t, child * rank:(child + 1) * rank, :] = lax.dot_general(
+                coupling_ref[child], masked, (((0,), (1,)), ((), ())),
+                preferred_element_type=jnp.float32,
             ).astype(jnp.bfloat16)
 
     for k in range(1, groups):
@@ -227,6 +242,25 @@
         diag_away.wait_send()
 
 
+def add_kernel(row_count, col_count, front_ref, rows_ref, cols_ref, diag_ref, out_ref):
+    cols_local, _, block = cols_ref.shape
+    halves = block // LANES
+    per_row = halves * cols_local
+    row_parent = pl.program_id(0) * row_count + lax.axis_index("row")
+    for b in range(cols_local):
+        tile = jnp.dot(rows_ref[...], cols_ref[b], preferred_element_type=jnp.float32)
+        for h in range(halves):
+            spot = pl.ds(h * cols_local + b, block, stride=per_row)
+            lanes = slice(h * LANES, (h + 1) * LANES)
+            out_ref[spot, :] = front_ref[spot, :] + tile[:, lanes]
+
+        @pl.when(row_parent == b * col_count + lax.axis_index("col"))
+        def _():
+            for h in range(halves):
+                spot = pl.ds(h * cols_local + b, block, stride=per_row)
+                out_ref[spot, :] = out_ref[spot, :] + diag_ref[b, :, h * LANES:(h + 1) * LANES]
+
+
 def shards(parent_front, generators, diagonal_blocks, coupling, block_map, valid_rows):
     row_count = lax.axis_size("row")
     col_count = lax.axis_size("col")
@@ -238,18 +272,24 @@
     col_cap = cols_local // groups
     chunk = row_cap * block // QUAD
     vmem = pl.BlockSpec(memory_space=pltpu.VMEM)
-    smem = pl.BlockSpec(memory_space=pltpu.SMEM)
+    hbm = pl.BlockSpec(memory_space=pltpu.HBM)
     dma = pltpu.SemaphoreType.DMA
     rows, cols, diag = pl.pallas_call(
         functools.partial(exchange_kernel, row_count, col_count, row_cap, col_cap),
         out_shape=(
             jax.ShapeDtypeStruct((groups, QUAD, chunk, 2 * rank), jnp.bfloat16),
-            jax.ShapeDtypeStruct((groups, col_cap, block, 2 * rank), jnp.bfloat16),
+            jax.ShapeDtypeStruct((groups, col_cap, 2 * rank, block), jnp.bfloat16),
             jax.ShapeDtypeStruct((groups, col_cap, block, block), jnp.float32),
         ),
-        in_specs=[vmem, vmem, vmem, smem, smem],
+        in_specs=[hbm] * 5,
         out_specs=(vmem, vmem, vmem),
         scratch_shapes=[
+            pltpu.VMEM(generators.shape, jnp.bfloat16),
+            pltpu.VMEM(diagonal_blocks.shape, jnp.bfloat16),
+            pltpu.VMEM(coupling.shape, jnp.bfloat16),
+            pltpu.SMEM(block_map.shape, jnp.int32),
+            pltpu.SMEM(valid_rows.shape, jnp.int32),
+            dma((5,)),
             pltpu.VMEM((groups - 1, 2, chunk, rank), jnp.bfloat16),
             pltpu.VMEM((row_cap * block, rank), jnp.bfloat16),
             pltpu.VMEM((2, groups, QUAD, chunk, rank), jnp.bfloat16),
@@ -269,18 +309,31 @@
             dma((2, groups)),
         ],
         compiler_params=pltpu.CompilerParams(
-            collective_id=0, has_side_effects=True, vmem_limit_bytes=48 * 1024 * 1024
+            collective_id=0, has_side_effects=True, vmem_limit_bytes=67_043_328
         ),
     )(generators, diagonal_blocks, coupling, block_map, valid_rows)
     rows = rows.reshape(rows_local, block, 2 * rank)
-    cols = cols.reshape(cols_local, block, 2 * rank)
+    cols = cols.reshape(cols_local, 2 * rank, block)
     diag = diag.reshape(cols_local, block, block)
-    row_parents = jnp.arange(rows_local, dtype=jnp.int32) * row_count + lax.axis_index("row")
-    col_parents = jnp.arange(cols_local, dtype=jnp.int32) * col_count + lax.axis_index("col")
-    on_diag = (row_parents[:, None] == col_parents[None, :]).astype(jnp.float32)
-    tiles = jnp.einsum("axq,bzq->axbz", rows, cols, preferred_element_type=jnp.float32)
-    placed = on_diag[:, None, :, None] * diag.transpose(1, 0, 2)[None]
-    return parent_front + (tiles + placed)
+    halves = block // LANES
+    per_row = halves * cols_local
+    flat = parent_front.reshape(rows_local, block, cols_local, halves, LANES)
+    flat = flat.transpose(0, 1, 3, 2, 4).reshape(rows_local, block * per_row, LANES)
+    flat_spec = pl.BlockSpec((None, block * per_row, LANES), lambda a: (a, 0, 0))
+    out = pl.pallas_call(
+        functools.partial(add_kernel, row_count, col_count),
+        grid=(rows_local,),
+        out_shape=jax.ShapeDtypeStruct(flat.shape, jnp.float32),
+        in_specs=[
+            flat_spec,
+            pl.BlockSpec((None, block, 2 * rank), lambda a: (a, 0, 0)),
+            pl.BlockSpec(cols.shape, lambda a: (0, 0, 0)),
+            pl.BlockSpec(diag.shape, lambda a: (0, 0, 0)),
+        ],
+        out_specs=flat_spec,
+    )(flat, rows, cols, diag)
+    out = out.reshape(rows_local, block, halves, cols_local, LANES)
+    return out.transpose(0, 1, 3, 2, 4).reshape(parent_front.shape)
 
 
 def solution(mesh):

time: 53.6 us -> 40.9 us (0.76)
  local copies, waits for them, and re-layouts: 17.3 us -> 0 us
  Pallas kernels: 25 us -> 40.6 us
  matrix products: 10.4 us -> 0 us
    pallas_call x0 -> x1, Pallas kernels: none -> 14.1 us  [shards(): pl.pallas_call(functools.partial(add_kernel, row_count, col_count), grid=...]
    add x1 -> x0, local copies, waits for them, and re-layouts: 12.2 us -> none  [shards(): return parent_front + (tiles + placed)]
    dot_general x1 -> x0, matrix products: 10.4 us -> none  [shards(): jnp.einsum('axq,bzq->axbz', rows, cols, preferred_element_type=jnp.float32)]
    unnamed x10 -> x0, local copies, waits for them, and re-layouts: 5.12 us -> none
    pallas_call x1, Pallas kernels: 25 us -> 26.5 us  [shards(): pl.pallas_call(functools.partial(exchange_kernel, row_count, col_count, r...]
where the time goes in v2:
time: 40.9 us; the launch traced here: 40.6 us
  Pallas kernels  40.6 us (99%)
    pallas_call x1, Pallas kernels, shards(): pl.pallas_call(functools.partial(exchange_kernel, row_count, col_count, r...  26.5 us
    pallas_call x1, Pallas kernels, shards(): pl.pallas_call(functools.partial(add_kernel, row_count, col_count), grid=...  14.1 us

profile of v2, /device:TPU:1, one launch (start us, length us, event | category | flops | bytes accessed | tf_op | source)
XLA Modules:
  0.0 40.6 jit_solution(9964570908956976801)
XLA Ops:
  0.0 26.5 %shard_map.64 = (bf16[2,4,256,512]{3,2,1,0:T(8,128)(2,1)}, bf16[2,2,512,256]{3,2,1,0:T(8,128)(2,1)}, f32[2,2,256,256]{3,2,1,0:T(8,128)}) custom-call(bf16[12,256,256]{2,1,0:T(8,128)(2,1)} %gen_hbm.1, bf16[12,256,256]{2,1,0:T(8,128)(2,1)} %diag_hbm.1, bf16[2,256,256]{2,1,0:T(8,128)(2,1)} %coupling_hbm.1, s32[2,24]{1,0:T(2,128)} %map_hbm.1, s32[2,24]{1,0:T(2,128)} %count_hbm.1), custom_call_target="tpu_custom_call" | custom-call | tf_op jit(solution)/shard_map/pallas_call | solution.py:277
  26.5 14.1 %shard_map.65 = f32[8,2048,128]{2,1,0:T(8,128)} custom-call(f32[8,2048,128]{2,1,0:T(8,128)} %bitcast.13, bf16[8,256,512]{2,1,0:T(8,128)(2,1)} %bitcast.14, bf16[4,512,256]{2,1,0:T(8,128)(2,1)} %bitcast.15, f32[4,256,256]{2,1,0:T(8,128)} %bitcast.16), custom_call_target="tpu_custom_call" | custom-call | tf_op jit(solution)/shard_map/pallas_call | solution.py:323

commit v3 on v2

--- a/solution.py
+++ b/solution.py
@@ -14,9 +14,9 @@
 
 def exchange_kernel(
     row_count, col_count, row_cap, col_cap,
-    gen_hbm, diag_hbm, coupling_hbm, map_hbm, count_hbm,
-    rows_out, cols_out, diag_out,
-    gen_ref, diag_ref, coupling_ref, map_ref, count_ref, load_sem,
+    gen_hbm, diag_hbm, coupling_hbm, map_hbm, count_hbm, front_hbm,
+    rows_out, cols_out, diag_out, front_out,
+    gen_ref, diag_ref, coupling_ref, map_ref, count_ref, load_sem, front_sem,
     send_rows, send_pair, rows_raw, cols_raw, diag_raw,
     far_send, far_recv, quad_send, quad_recv, pair_send, pair_recv,
     col_send, col_recv, fwd_send, fwd_recv, diag_send, diag_recv,
@@ -74,6 +74,8 @@
 
     for load in loads:
         load.wait()
+    front_load = pltpu.make_async_copy(front_hbm, front_out, front_sem)
+    front_load.start()
     start_row = quarter * chunk
     quarter_slot = start_row // block
     quarter_off = pl.multiple_of(start_row % block, chunk)
@@ -234,6 +236,7 @@
             for j in range(QUAD):
                 finish_rows(child, source, j)
 
+    front_load.wait()
     for copy in sends:
         copy.wait_send()
 
@@ -242,23 +245,40 @@
         diag_away.wait_send()
 
 
-def add_kernel(row_count, col_count, front_ref, rows_ref, cols_ref, diag_ref, out_ref):
+def add_kernel(
+    row_count, col_count, front_ref, rows_ref, cols_ref, diag_ref, out_ref, staged, out_sem
+):
+    rows_local = rows_ref.shape[0]
     cols_local, _, block = cols_ref.shape
     halves = block // LANES
     per_row = halves * cols_local
-    row_parent = pl.program_id(0) * row_count + lax.axis_index("row")
-    for b in range(cols_local):
-        tile = jnp.dot(rows_ref[...], cols_ref[b], preferred_element_type=jnp.float32)
-        for h in range(halves):
-            spot = pl.ds(h * cols_local + b, block, stride=per_row)
-            lanes = slice(h * LANES, (h + 1) * LANES)
-            out_ref[spot, :] = front_ref[spot, :] + tile[:, lanes]
-
-        @pl.when(row_parent == b * col_count + lax.axis_index("col"))
-        def _():
+    row = lax.axis_index("row")
+    col = lax.axis_index("col")
+
+    def write(a):
+        return pltpu.make_async_copy(staged.at[a % 2], out_ref.at[a], out_sem.at[a % 2])
+
+    for a in range(rows_local):
+        if a >= 2:
+            write(a - 2).wait()
+        for b in range(cols_local):
+            tile = jnp.dot(rows_ref[a], cols_ref[b], preferred_element_type=jnp.float32)
             for h in range(halves):
                 spot = pl.ds(h * cols_local + b, block, stride=per_row)
-                out_ref[spot, :] = out_ref[spot, :] + diag_ref[b, :, h * LANES:(h + 1) * LANES]
+                staged[a % 2, spot, :] = front_ref[a, spot, :] + tile[:, h * LANES:(h + 1) * LANES]
+        row_parent = a * row_count + row
+
+        @pl.when(row_parent % col_count == col)
+        def _():
+            b = row_parent // col_count
+            for h in range(halves):
+                spot = pl.ds(h * cols_local + b, block, stride=per_row)
+                piece = diag_ref[b, :, h * LANES:(h + 1) * LANES]
+                staged[a % 2, spot, :] = staged[a % 2, spot, :] + piece
+
+        write(a).start()
+    for a in range(rows_local - 2, rows_local):
+        write(a).wait()
 
 
 def shards(parent_front, generators, diagonal_blocks, coupling, block_map, valid_rows):
@@ -274,15 +294,24 @@
     vmem = pl.BlockSpec(memory_space=pltpu.VMEM)
     hbm = pl.BlockSpec(memory_space=pltpu.HBM)
     dma = pltpu.SemaphoreType.DMA
-    rows, cols, diag = pl.pallas_call(
+    halves = block // LANES
+    per_row = halves * cols_local
+    flat = parent_front.reshape(rows_local, block, cols_local, halves, LANES)
+    flat = flat.transpose(0, 1, 3, 2, 4).reshape(rows_local, block * per_row, LANES)
+    operands = [
+        pltpu.with_memory_space_constraint(x, pltpu.HBM)
+        for x in (generators, diagonal_blocks, coupling, block_map, valid_rows, flat)
+    ]
+    rows, cols, diag, front = pl.pallas_call(
         functools.partial(exchange_kernel, row_count, col_count, row_cap, col_cap),
         out_shape=(
-            jax.ShapeDtypeStruct((groups, QUAD, chunk, 2 * rank), jnp.bfloat16),
-            jax.ShapeDtypeStruct((groups, col_cap, 2 * rank, block), jnp.bfloat16),
-            jax.ShapeDtypeStruct((groups, col_cap, block, block), jnp.float32),
+            pltpu.VMEM((groups, QUAD, chunk, 2 * rank), jnp.bfloat16),
+            pltpu.VMEM((groups, col_cap, 2 * rank, block), jnp.bfloat16),
+            pltpu.VMEM((groups, col_cap, block, block), jnp.float32),
+            pltpu.VMEM(flat.shape, jnp.float32),
         ),
-        in_specs=[hbm] * 5,
-        out_specs=(vmem, vmem, vmem),
+        in_specs=[hbm] * 6,
+        out_specs=(vmem,) * 4,
         scratch_shapes=[
             pltpu.VMEM(generators.shape, jnp.bfloat16),
             pltpu.VMEM(diagonal_blocks.shape, jnp.bfloat16),
@@ -290,6 +319,7 @@
             pltpu.SMEM(block_map.shape, jnp.int32),
             pltpu.SMEM(valid_rows.shape, jnp.int32),
             dma((5,)),
+            dma,
             pltpu.VMEM((groups - 1, 2, chunk, rank), jnp.bfloat16),
             pltpu.VMEM((row_cap * block, rank), jnp.bfloat16),
             pltpu.VMEM((2, groups, QUAD, chunk, rank), jnp.bfloat16),
@@ -309,29 +339,20 @@
             dma((2, groups)),
         ],
         compiler_params=pltpu.CompilerParams(
-            collective_id=0, has_side_effects=True, vmem_limit_bytes=67_043_328
+            collective_id=0, has_side_effects=True, vmem_limit_bytes=32 * 1024 * 1024
         ),
-    )(generators, diagonal_blocks, coupling, block_map, valid_rows)
+    )(*operands)
     rows = rows.reshape(rows_local, block, 2 * rank)
     cols = cols.reshape(cols_local, 2 * rank, block)
     diag = diag.reshape(cols_local, block, block)
-    halves = block // LANES
-    per_row = halves * cols_local
-    flat = parent_front.reshape(rows_local, block, cols_local, halves, LANES)
-    flat = flat.transpose(0, 1, 3, 2, 4).reshape(rows_local, block * per_row, LANES)
-    flat_spec = pl.BlockSpec((None, block * per_row, LANES), lambda a: (a, 0, 0))
     out = pl.pallas_call(
         functools.partial(add_kernel, row_count, col_count),
-        grid=(rows_local,),
         out_shape=jax.ShapeDtypeStruct(flat.shape, jnp.float32),
-        in_specs=[
-            flat_spec,
-            pl.BlockSpec((None, block, 2 * rank), lambda a: (a, 0, 0)),
-            pl.BlockSpec(cols.shape, lambda a: (0, 0, 0)),
-            pl.BlockSpec(diag.shape, lambda a: (0, 0, 0)),
-        ],
-        out_specs=flat_spec,
-    )(flat, rows, cols, diag)
+        in_specs=[vmem] * 4,
+        out_specs=hbm,
+        scratch_shapes=[pltpu.VMEM((2,) + flat.shape[1:], jnp.float32), dma((2,))],
+        compiler_params=pltpu.CompilerParams(vmem_limit_bytes=32 * 1024 * 1024),
+    )(*(pltpu.with_memory_space_constraint(x, pltpu.VMEM) for x in (front, rows, cols, diag)))
     out = out.reshape(rows_local, block, halves, cols_local, LANES)
     return out.transpose(0, 1, 3, 2, 4).reshape(parent_front.shape)
 

time: 40.9 us -> 31.3 us (0.77)
  Pallas kernels: 40.6 us -> 31.1 us
    pallas_call x1, Pallas kernels: 14.1 us -> 6.61 us  [shards(): pl.pallas_call(functools.partial(add_kernel, row_count, col_count), out_s...]
    pallas_call x1, Pallas kernels: 26.5 us -> 24.5 us  [shards(): pl.pallas_call(functools.partial(exchange_kernel, row_count, col_count, r...]
where the time goes in v3:
time: 31.3 us; the launch traced here: 31.1 us
  Pallas kernels  31.1 us (99%)
    pallas_call x1, Pallas kernels, shards(): pl.pallas_call(functools.partial(exchange_kernel, row_count, col_count, r...  24.5 us
    pallas_call x1, Pallas kernels, shards(): pl.pallas_call(functools.partial(add_kernel, row_count, col_count), out_s...  6.61 us

profile of v3, /device:TPU:1, one launch (start us, length us, event | category | flops | bytes accessed | tf_op | source)
XLA Modules:
  0.0 31.1 jit_solution(4828564964532914909)
XLA Ops:
  0.0 24.5 %shard_map.64 = (bf16[2,4,256,512]{3,2,1,0:T(8,128)(2,1)S(1)}, bf16[2,2,512,256]{3,2,1,0:T(8,128)(2,1)S(1)}, f32[2,2,256,256]{3,2,1,0:T(8,128)S(1)}, f32[8,2048,128]{2,1,0:T(8,128)S(1)}) custom-call(bf16[12,256,256]{2,1,0:T(8,128)(2,1)} %gen_hbm.1, bf16[12,256,256]{2,1,0:T(8,128)(2,1)} %diag_hbm.1, bf16[2,256,256]{2,1,0:T(8,128)(2,1)} %coupling_hbm.1, ...), custom_call_target="tpu_custom_call" | custom-call | tf_op jit(solution)/shard_map/pallas_call | solution.py:305
  24.5 6.6 %shard_map.65 = f32[8,2048,128]{2,1,0:T(8,128)} custom-call(f32[8,2048,128]{2,1,0:T(8,128)S(1)} %get-tuple-element.9.front_ref, bf16[8,256,512]{2,1,0:T(8,128)(2,1)S(1)} %bitcast.13, bf16[4,512,256]{2,1,0:T(8,128)(2,1)S(1)} %bitcast.14, f32[4,256,256]{2,1,0:T(8,128)S(1)} %bitcast.15), custom_call_target="tpu_custom_call" | custom-call | tf_op jit(solution)/shard_map/pallas_call | solution.py:348

commit v4 on v3

--- a/solution.py
+++ b/solution.py
@@ -19,7 +19,7 @@
     gen_ref, diag_ref, coupling_ref, map_ref, count_ref, load_sem, front_sem,
     send_rows, send_pair, rows_raw, cols_raw, diag_raw,
     far_send, far_recv, quad_send, quad_recv, pair_send, pair_recv,
-    col_send, col_recv, fwd_send, fwd_recv, diag_send, diag_recv,
+    col_send, col_recv, fwd_send, fwd_recv, diag_send, diag_recv, own_send, own_recv,
 ):
     groups = row_count // 2
     group_blocks, block, rank = gen_ref.shape
@@ -107,11 +107,12 @@
             sends.append(copy)
 
     own_cols = cols_raw.at[core, group]
+    col_away = []
     for k in range(1, groups):
         dest = (group + k) % groups
         copy = remote(own_cols, own_cols, col_send.at[k], col_recv.at[k], 2 * dest + core, col)
-        copy.start()
-        sends.append(copy)
+        pl.when(diag_row // 2 != dest)(copy.start)
+        col_away.append((dest, copy))
     copy = remote(own_cols, own_cols, col_send.at[0], col_recv.at[0], pair_row, col)
     copy.start()
     sends.append(copy)
@@ -184,20 +185,25 @@
     for child in range(2):
         finish_cols(child, group)
 
-    for k in range(1, groups):
-        source = (group + groups - k) % groups
-        landed = cols_raw.at[core, source]
-        remote(own_cols, landed, col_send.at[k], col_recv.at[k], pair_row, col).wait_recv()
-        copy = remote(landed, landed, fwd_send.at[k - 1], fwd_recv.at[k - 1], pair_row, col)
-        copy.start()
-        sends.append(copy)
-    for k in range(1, groups):
-        source = (group + groups - k) % groups
-        remote(
-            own_cols, cols_raw.at[1 - core, source], fwd_send.at[k - 1], fwd_recv.at[k - 1], pair_row, col
-        ).wait_recv()
-        for child in range(2):
-            finish_cols(child, source)
+    far_sources = [(k, (group + groups - k) % groups) for k in range(1, groups)]
+
+    @pl.when(diag_row // 2 != group)
+    def _():
+        shared = []
+        for k, source in far_sources:
+            landed = cols_raw.at[core, source]
+            remote(own_cols, landed, col_send.at[k], col_recv.at[k], pair_row, col).wait_recv()
+            shared.append(remote(
+                landed, landed, fwd_send.at[k - 1], fwd_recv.at[k - 1], pair_row, col
+            ))
+            shared[-1].start()
+        for k, source in far_sources:
+            remote(
+                own_cols, cols_raw.at[1 - core, source], fwd_send.at[k - 1], fwd_recv.at[k - 1],
+                pair_row, col,
+            ).wait_recv()
+        for copy in shared:
+            copy.wait_send()
 
     @pl.when(row == diag_row)
     def _():
@@ -232,13 +238,47 @@
                     landed, landed, quad_send.at[k - 1, child, j], quad_recv.at[k - 1, child, j],
                     row, other,
                 ).wait_recv()
+
+    @pl.when(diag_row // 2 == group)
+    def _():
+        pieces = block // chunk
+        shared = []
+        for k, source in far_sources:
+            for child in range(2):
+                for n in range(col_cap * pieces):
+                    slot = (n // pieces * col_count + col) // row_count
+                    landed = rows_raw.at[child, source, slot * pieces + n % pieces]
+                    spot = cols_raw.at[child, source, pl.ds(n * chunk, chunk)]
+                    shared.append((landed, spot, remote(
+                        landed, spot, own_send.at[k - 1, child, n], own_recv.at[k - 1, child, n],
+                        pair_row, col,
+                    )))
+
+        @pl.when(row == diag_row)
+        def _():
+            for landed, spot, copy in shared:
+                copy.start()
+            for landed, spot, copy in shared:
+                spot[...] = landed[...]
+            for landed, spot, copy in shared:
+                copy.wait_send()
+
+        @pl.when(row != diag_row)
+        def _():
+            for landed, spot, copy in shared:
+                copy.wait_recv()
+
+    for k, source in far_sources:
         for child in range(2):
+            finish_cols(child, source)
             for j in range(QUAD):
                 finish_rows(child, source, j)
 
     front_load.wait()
     for copy in sends:
         copy.wait_send()
+    for dest, copy in col_away:
+        pl.when(diag_row // 2 != dest)(copy.wait_send)
 
     @pl.when(row != diag_row)
     def _():
@@ -337,6 +377,8 @@
             dma((groups - 1,)),
             dma,
             dma((2, groups)),
+            dma((groups - 1, 2, col_cap * block // chunk)),
+            dma((groups - 1, 2, col_cap * block // chunk)),
         ],
         compiler_params=pltpu.CompilerParams(
             collective_id=0, has_side_effects=True, vmem_limit_bytes=32 * 1024 * 1024

time: 31.3 us -> 32.1 us (1.026)
  Pallas kernels: 31.1 us -> 31.6 us
    pallas_call x1, Pallas kernels: 24.5 us -> 25 us  [shards(): pl.pallas_call(functools.partial(exchange_kernel, row_count, col_count, r...]
where the time goes in v4:
time: 32.1 us; the launch traced here: 31.6 us
  Pallas kernels  31.6 us (98%)
    pallas_call x1, Pallas kernels, shards(): pl.pallas_call(functools.partial(exchange_kernel, row_count, col_count, r...  25 us
    pallas_call x1, Pallas kernels, shards(): pl.pallas_call(functools.partial(add_kernel, row_count, col_count), out_s...  6.61 us

profile of v4, /device:TPU:1, one launch (start us, length us, event | category | flops | bytes accessed | tf_op | source)
XLA Modules:
  0.0 31.6 jit_solution(3088529978452271233)
XLA Ops:
  0.0 25.0 %shard_map.64 = (bf16[2,4,256,512]{3,2,1,0:T(8,128)(2,1)S(1)}, bf16[2,2,512,256]{3,2,1,0:T(8,128)(2,1)S(1)}, f32[2,2,256,256]{3,2,1,0:T(8,128)S(1)}, f32[8,2048,128]{2,1,0:T(8,128)S(1)}) custom-call(bf16[12,256,256]{2,1,0:T(8,128)(2,1)} %gen_hbm.1, bf16[12,256,256]{2,1,0:T(8,128)(2,1)} %diag_hbm.1, bf16[2,256,256]{2,1,0:T(8,128)(2,1)} %coupling_hbm.1, ...), custom_call_target="tpu_custom_call" | custom-call | tf_op jit(solution)/shard_map/pallas_call | solution.py:345
  25.0 6.6 %shard_map.65 = f32[8,2048,128]{2,1,0:T(8,128)} custom-call(f32[8,2048,128]{2,1,0:T(8,128)S(1)} %get-tuple-element.9.front_ref, bf16[8,256,512]{2,1,0:T(8,128)(2,1)S(1)} %bitcast.13, bf16[4,512,256]{2,1,0:T(8,128)(2,1)S(1)} %bitcast.14, f32[4,256,256]{2,1,0:T(8,128)S(1)} %bitcast.15), custom_call_target="tpu_custom_call" | custom-call | tf_op jit(solution)/shard_map/pallas_call | solution.py:390
